TPU v7x, 32 devices: a whole 2x2x4 slice. The times are simulated.
32 devices in a mesh: dp: 8 (over y, x, core), tm: 4 (over z).
Axes of the slice: x: 2, y: 2, z: 4, core: 2. Of those that a mesh axis runs over, the one named last changes fastest.
Arguments:
- audio: float32 [24, 8, 1024], P('dp', None, 'tm'), may hold values from -3.15 to 3.15, as said below
- mel_frames: bfloat16 [24, 1024, 640], P('dp', 'tm'), may hold values from -6 to 6
- start_weight: float32 [4, 512], replicated, may hold values from -3 to 3
- input_weight: bfloat16 [2, 3, 512, 1024], replicated, may hold values from -0.15625 to 0.15625
- cond_weight: bfloat16 [2, 640, 1024], replicated, may hold values from -0.25 to 0.25
- res_weight: bfloat16 [1, 512, 1024], replicated, may hold values from -0.25 to 0.25
- last_weight: bfloat16 [512, 512], replicated, may hold values from -0.25 to 0.25
- end_weight: bfloat16 [512, 8], replicated, may hold values from -0.25 to 0.25
Outputs:
- latent: float32 [24, 4, 1024], P('dp', None, 'tm')
- audio_grad: float32 [24, 8, 1024], P('dp', None, 'tm')
- batch_loss: float32 [], replicated
- input_weight_grad: float32 [2, 3, 512, 1024], P(None, None, 'dp', 'tm')
- cond_weight_grad: float32 [2, 640, 1024], P(None, 'dp', 'tm')
- res_weight_grad: float32 [1, 512, 1024], P(None, 'dp', 'tm')
- last_weight_grad: float32 [512, 512], replicated
- end_weight_grad: float32 [512, 8], replicated
- start_weight_grad: float32 [4, 512], replicated
Inputs may be any that keep to these rules, and one draw needn't show every extreme that they name: `audio`: audio samples.
All inputs are finite; a program needn't handle non-finite values.
Results may differ from a plain program's by a relative error of at most 0.015.
Values may be sent and summed in bfloat16 or wider, within the bound.
A program may use at most 128 MiB of HBM per device.

v0:
```python
import jax
import jax.numpy as jnp
from jax import lax
from jax.sharding import PartitionSpec as P

highest = lax.Precision.HIGHEST


def with_halo(block, sides, width):
    for axis, dim in sides:
        count = lax.axis_size(axis)
        forward = [(i, i + 1) for i in range(count - 1)]
        backward = [(target, source) for source, target in forward]
        low = lax.ppermute(
            lax.slice_in_dim(block, block.shape[dim] - width, None, axis=dim), axis, forward
        )
        high = lax.ppermute(lax.slice_in_dim(block, 0, width, axis=dim), axis, backward)
        block = jnp.concatenate([low, block, high], axis=dim)
    return block


def gated_unit(pre_act, channels):
    return jnp.tanh(pre_act[..., :channels]) * jax.nn.sigmoid(pre_act[..., channels:])


def gated_back(pre_act, upstream, channels):
    tangent = jnp.tanh(pre_act[..., :channels])
    switch = jax.nn.sigmoid(pre_act[..., channels:])
    return jnp.concatenate(
        [
            upstream * (1.0 - tangent * tangent) * switch,
            upstream * tangent * switch * (1.0 - switch),
        ],
        axis=-1,
    )


def project(values, weight):
    return jnp.einsum("cti,io->cto", values, weight, preferred_element_type=jnp.float32)


def dilated(padded, weight, spread, length):
    summed = None
    for tap_index in range(weight.shape[0]):
        window = padded[:, tap_index * spread : tap_index * spread + length]
        tap_term = project(window, weight[tap_index])
        summed = tap_term if summed is None else summed + tap_term
    return summed


def dilated_back(padded_grad, weight, spread, length):
    taps = weight.shape[0]
    summed = None
    for tap_index in range(taps):
        offset = (taps - 1 - tap_index) * spread
        window = padded_grad[:, offset : offset + length]
        tap_term = jnp.einsum(
            "cto,io->cti", window, weight[tap_index], preferred_element_type=jnp.float32
        )
        summed = tap_term if summed is None else summed + tap_term
    return summed


def shards(
    audio, mel_frames, start_weight, input_weight, cond_weight, res_weight, last_weight, end_weight
):
    clips_dev, group_size, frames_dev = audio.shape
    half_group = group_size // 2
    channels = start_weight.shape[1]
    layers = input_weight.shape[0]
    taps = input_weight.shape[1]
    scale_inv = 1.0 / (clips_dev * lax.axis_size("dp"))
    first_half = jnp.transpose(audio[:, :half_group], (0, 2, 1))
    second_half = jnp.transpose(audio[:, half_group:], (0, 2, 1))
    stored = []
    skip_sum = jnp.zeros((clips_dev, frames_dev, channels), jnp.float32)
    hidden = jnp.einsum("cth,hk->ctk", first_half, start_weight, precision=highest)
    for layer_index in range(layers):
        spread = 2**layer_index
        padded = with_halo(hidden.astype(jnp.bfloat16), (("tm", 1),), spread)
        pre_act = dilated(padded, input_weight[layer_index], spread, frames_dev) + project(
            mel_frames, cond_weight[layer_index]
        )
        gated_out = gated_unit(pre_act, channels).astype(jnp.bfloat16)
        stored.append((padded, pre_act, gated_out))
        if layer_index < layers - 1:
            mixed = project(gated_out, res_weight[layer_index])
            hidden = hidden + mixed[..., :channels]
            skip_sum = mixed[..., channels:]
        else:
            skip_sum = skip_sum + project(gated_out, last_weight)
    skip_b = skip_sum.astype(jnp.bfloat16)
    outputs = project(skip_b, end_weight)
    log_scale = outputs[..., :half_group]
    shift_term = outputs[..., half_group:]
    growth = jnp.exp(log_scale)
    latent_rows = growth * second_half + shift_term
    local_loss = (
        0.5 * jnp.sum(first_half * first_half)
        + 0.5 * jnp.sum(latent_rows * latent_rows)
        - jnp.sum(log_scale)
    ) * scale_inv
    batch_loss = lax.psum(local_loss, ("dp", "tm"))
    grad_out = jnp.concatenate(
        [(latent_rows * growth * second_half - 1.0) * scale_inv, latent_rows * scale_inv], axis=-1
    ).astype(jnp.bfloat16)
    end_grad = jnp.einsum("cti,ctg->ig", skip_b, grad_out, preferred_element_type=jnp.float32)
    skip_back = jnp.einsum(
        "ctg,ig->cti", grad_out, end_weight, preferred_element_type=jnp.float32
    ).astype(jnp.bfloat16)
    state_back = jnp.zeros((clips_dev, frames_dev, channels), jnp.float32)
    in_grads = [None] * layers
    cond_grads = [None] * layers
    res_grads = [None] * (layers - 1)
    last_grad = None
    upper_sums = None
    for layer_index in reversed(range(layers)):
        spread = 2**layer_index
        padded, pre_act, gated_out = stored[layer_index]
        if layer_index == layers - 1:
            act_back = jnp.einsum(
                "ctj,ij->cti", skip_back, last_weight, preferred_element_type=jnp.float32
            )
            last_grad = jnp.einsum(
                "cti,ctj->ij", gated_out, skip_back, preferred_element_type=jnp.float32
            )
        else:
            joined = jnp.concatenate([state_back.astype(jnp.bfloat16), skip_back], axis=-1)
            act_back = jnp.einsum(
                "ctj,ij->cti", joined, res_weight[layer_index], preferred_element_type=jnp.float32
            )
            res_grads[layer_index] = jnp.einsum(
                "cti,ctj->ij", gated_out, joined, preferred_element_type=jnp.float32
            )
        pre_back = gated_back(pre_act, act_back, channels).astype(jnp.bfloat16)
        in_grads[layer_index] = jnp.stack(
            [
                jnp.einsum(
                    "cti,cto->io",
                    padded[:, tap_index * spread : tap_index * spread + frames_dev],
                    pre_back,
                    preferred_element_type=jnp.float32,
                )
                for tap_index in range(taps)
            ]
        )
        cond_grads[layer_index] = jnp.einsum(
            "ctm,cto->mo", mel_frames, pre_back, preferred_element_type=jnp.float32
        )
        grad_pad = with_halo(pre_back, (("tm", 1),), spread)
        state_back = state_back + dilated_back(
            grad_pad, input_weight[layer_index], spread, frames_dev
        )
        if layer_index == layers - 1:
            upper_part = (
                lax.psum_scatter(
                    in_grads[layer_index].astype(jnp.bfloat16),
                    "tm",
                    scatter_dimension=2,
                    tiled=True,
                ).astype(jnp.float32),
                lax.psum_scatter(
                    cond_grads[layer_index].astype(jnp.bfloat16),
                    "tm",
                    scatter_dimension=1,
                    tiled=True,
                ).astype(jnp.float32),
            )
            upper_sums = (
                lax.psum_scatter(
                    upper_part[0].astype(jnp.bfloat16), "dp", scatter_dimension=1, tiled=True
                ).astype(jnp.float32),
                lax.psum_scatter(
                    upper_part[1].astype(jnp.bfloat16), "dp", scatter_dimension=0, tiled=True
                ).astype(jnp.float32),
            )
    start_grad = jnp.einsum("cth,ctk->hk", first_half, state_back, precision=highest)
    first_back = (
        jnp.einsum("ctk,hk->cth", state_back, start_weight, precision=highest)
        + first_half * scale_inv
    )
    audio_grad = jnp.transpose(
        jnp.concatenate([first_back, latent_rows * growth * scale_inv], axis=-1), (0, 2, 1)
    )
    latent = jnp.transpose(latent_rows, (0, 2, 1))
    lower_part = (
        lax.psum_scatter(jnp.stack(in_grads[:-1]), "tm", scatter_dimension=3, tiled=True),
        lax.psum_scatter(jnp.stack(cond_grads[:-1]), "tm", scatter_dimension=2, tiled=True),
        lax.psum_scatter(jnp.stack(res_grads), "tm", scatter_dimension=2, tiled=True),
    )
    lower_sums = (
        lax.psum_scatter(lower_part[0], "dp", scatter_dimension=2, tiled=True),
        lax.psum_scatter(lower_part[1], "dp", scatter_dimension=1, tiled=True),
        lax.psum_scatter(lower_part[2], "dp", scatter_dimension=1, tiled=True),
    )
    in_grad = jnp.concatenate([lower_sums[0], upper_sums[0][None]], axis=0)
    cond_grad = jnp.concatenate([lower_sums[1], upper_sums[1][None]], axis=0)
    res_grad = lower_sums[2]
    last_total, end_total, start_total = lax.psum((last_grad, end_grad, start_grad), ("dp", "tm"))
    return (
        latent,
        audio_grad,
        batch_loss,
        in_grad,
        cond_grad,
        res_grad,
        last_total,
        end_total,
        start_total,
    )


def solution(mesh):
    return jax.shard_map(
        shards,
        mesh=mesh,
        in_specs=(P("dp", None, "tm"), P("dp", "tm", None), P(), P(), P(), P(), P(), P()),
        out_specs=(
            P("dp", None, "tm"),
            P("dp", None, "tm"),
            P(),
            P(None, None, "dp", "tm"),
            P(None, "dp", "tm"),
            P(None, "dp", "tm"),
            P(),
            P(),
            P(),
        ),
        check_vma=False,
    )
```

profile of v0, /device:TPU:0, one launch (start us, length us, event | category | flops | bytes accessed | tf_op | source)
XLA Modules:
  0.0 708.9 jit_solution(10755058474911952331)
XLA Ops:
  7.2 2.3 fusion.106
  11.0 5.8 collective-permute-start
  16.8 3.0 fusion.20
  27.4 3.9 collective-permute-start.2
  34.8 3.0 collective-permute-done.3
  44.5 2.5 fusion.16
  51.6 4.5 collective-permute-start.5
  58.5 3.6 fusion.107
  64.8 2.9 convolution_bitcast_fusion
  68.1 2.5 fusion.17
  79.1 3.3 maximum_bitcast_fusion
  83.7 3.5 convolution_bitcast_fusion.1
  89.2 42.2 %reduce-scatter.20.cloned.1.call-done = f32[1,640,256]{1,2,0:T(8,128)} async-done(((f32[1,640,1024]{1,2,0:T(8,128)}), f32[1,640,256]{1,2,0:T(8,128)}) %reduce-scatter.20.cloned.1.call-update) | async-done | bytes 655376 | tf_op jit(solution)/shard_map/reduce_scatter | solution.py:188
  133.5 60.1 %reduce-scatter.16.cloned.1.call-done = bf16[3,512,256]{2,1,0:T(8,128)(2,1)} async-done(((bf16[3,512,1024]{2,1,0:T(8,128)(2,1)}), bf16[3,512,256]{2,1,0:T(8,128)(2,1)}) %reduce-scatter.16.cloned.1.call-update) | async-done | bytes 786448 | tf_op jit(solution)/shard_map/reduce_scatter | solution.py:156
  193.7 112.8 %reduce-scatter.12.cloned.1.call-done = f32[1,3,512,256]{3,2,1,0:T(8,128)} async-done(((f32[1,3,512,1024]{3,2,1,0:T(8,128)}), f32[1,3,512,256]{3,2,1,0:T(8,128)}) %reduce-scatter.12.cloned.1.call-update) | async-done | bytes 1572880 | tf_op jit(solution)/shard_map/reduce_scatter | solution.py:187
  315.2 5.0 collective-permute-start.7
  322.5 2.3 add_add_fusion.2
  325.7 27.2 %reduce-scatter.24.cloned.1.call-done = f32[1,512,256]{2,1,0:T(8,128)} async-done(((f32[1,512,1024]{2,1,0:T(8,128)}), f32[1,512,256]{2,1,0:T(8,128)}) %reduce-scatter.24.cloned.1.call-update) | async-done | bytes 524304 | tf_op jit(solution)/shard_map/reduce_scatter | solution.py:189
  354.3 39.9 %all-reduce.1 = (f32[]{:T(128)}, f32[512,8]{0,1:T(8,128)}, f32[4,512]{1,0:T(4,128)}) all-reduce(f32[]{:T(128)S(6)} %mul.101, f32[512,8]{0,1:T(8,128)S(1)} %convolution_bitcast_fusion.6, f32[4,512]{1,0:T(4,128)S(1)} %convolution_bitcast_fusion.7), channel_id=1, replica_groups=mesh['dp'=8,'tm'=4] {'dp','tm'}, use_global_device_ids=true, to_apply=%region_3.0 | all-reduce | flops 6145 | bytes 49160 | tf_op jit(solution)/shard_map/psum | solution.py:103
  395.7 52.2 %all-reduce.7.cloned.1.call-done = f32[1,640,256]{2,0,1:T(1,128)} async-done(((f32[1,640,256]{2,0,1:T(1,128)}), f32[1,640,256]{2,0,1:T(1,128)}) %all-reduce.7.cloned.1.call-update) | async-done | bytes 655376
  449.6 35.7 %reduce-scatter.18.cloned.1.call-done = bf16[3,64,256]{2,1,0:T(8,128)(2,1)} async-done(((bf16[3,512,256]{2,1,0:T(8,128)(2,1)}), bf16[3,64,256]{2,1,0:T(8,128)(2,1)}) %reduce-scatter.18.cloned.1.call-update) | async-done | bytes 98320 | tf_op jit(solution)/shard_map/reduce_scatter | solution.py:170
  486.2 40.8 %reduce-scatter.14.cloned.1.call-done = f32[1,3,64,256]{3,2,1,0:T(8,128)} async-done(((f32[1,3,512,256]{3,2,1,0:T(8,128)}), f32[1,3,64,256]{3,2,1,0:T(8,128)}) %reduce-scatter.14.cloned.1.call-update) | async-done | bytes 196624 | tf_op jit(solution)/shard_map/reduce_scatter | solution.py:192
  528.7 134.6 %all-reduce.5.cloned.1.call-done = f32[512,512]{1,0:T(8,128)} async-done(((f32[512,512]{1,0:T(8,128)}), f32[512,512]{1,0:T(8,128)}) %all-reduce.5.cloned.1.call-update) | async-done | bytes 1048592 | tf_op jit(solution)/shard_map/psum | solution.py:199
  663.3 36.8 %reduce-scatter.26.cloned.1.call-done = f32[1,64,256]{2,1,0:T(8,128)} async-done(((f32[1,512,256]{2,1,0:T(8,128)}), f32[1,64,256]{2,1,0:T(8,128)}) %reduce-scatter.26.cloned.1.call-update) | async-done | bytes 65552 | tf_op jit(solution)/shard_map/reduce_scatter | solution.py:194
  (155 shorter events, 61.3 us)
Async XLA Ops:
  7.2 18.8 %copy-start = (bf16[1,512,1024]{2,1,0:T(8,128)(2,1)S(1)}, bf16[1,512,1024]{2,1,0:T(8,128)(2,1)}, u32[]{:S(2)}) copy-start(bf16[1,512,1024]{2,1,0:T(8,128)(2,1)} %param.13) | copy-start | bytes 3145732
  7.2 80.0 %reduce-scatter.22.cloned.1.call-start = ((), (), s32[]{:S(2)}) async-start(), calls=%async_computation.14 | async-start | bytes 1638400 | tf_op jit(solution)/shard_map/reduce_scatter | solution.py:162
  9.6 13.6 %collective-permute-start.1 = (bf16[3,1,512]{2,1,0:T(2,128)(2,1)S(1)}, bf16[3,1,512]{2,1,0:T(2,128)(2,1)S(1)}, u32[]{:S(2)}, u32[]{:S(2)}) collective-permute-start(bf16[3,1,512]{2,1,0:T(2,128)(2,1)S(1)} %get-tuple-element.42), channel_id=1, source_target_pairs={{1,0},{2,1},{3,2},{5,4},{6,5},{7,6},{9,8},{10,9},{11,10},{13,12},{... | collective-permute-start | bytes 9224 | tf_op jit(solution)/shard_map/ppermute | solution.py:17
  11.0 11.3 %collective-permute-start = (bf16[3,1,512]{2,1,0:T(2,128)(2,1)S(1)}, bf16[3,1,512]{2,1,0:T(2,128)(2,1)S(1)}, u32[]{:S(2)}, u32[]{:S(2)}) collective-permute-start(bf16[3,1,512]{2,1,0:T(2,128)(2,1)S(1)} %get-tuple-element.43), channel_id=1, source_target_pairs={{0,1},{1,2},{2,3},{4,5},{5,6},{6,7},{8,9},{9,10},{10,11},{12,13},{... | collective-permute-start | bytes 9224 | tf_op jit(solution)/shard_map/ppermute | solution.py:14
  27.4 6.4 collective-permute-start.2
  32.3 5.5 collective-permute-start.3
  47.1 84.3 %reduce-scatter.20.cloned.1.call-start = ((), (), s32[]{:S(2)}) async-start(), calls=%async_computation.13 | async-start | bytes 3276800 | tf_op jit(solution)/shard_map/reduce_scatter | solution.py:188
  48.1 8.1 %collective-permute-start.4 = (bf16[3,2,1024]{2,1,0:T(2,128)(2,1)S(1)}, bf16[3,2,1024]{2,1,0:T(2,128)(2,1)S(1)}, u32[]{:S(2)}, u32[]{:S(2)}) collective-permute-start(bf16[3,2,1024]{2,1,0:T(2,128)(2,1)S(1)} %get-tuple-element.39), channel_id=1, source_target_pairs={{1,0},{2,1},{3,2},{5,4},{6,5},{7,6},{9,8},{10,9},{11,10},{13,12},{... | collective-permute-start | bytes 36872 | tf_op jit(solution)/shard_map/ppermute | solution.py:17
  51.6 6.8 collective-permute-start.5
  67.8 125.9 %reduce-scatter.16.cloned.1.call-start = ((), (), s32[]{:S(2)}) async-start(), calls=%async_computation.11 | async-start | bytes 3932160 | tf_op jit(solution)/shard_map/reduce_scatter | solution.py:156
  74.7 231.8 %reduce-scatter.12.cloned.1.call-start = ((), (), s32[]{:S(2)}) async-start(), calls=%async_computation.9 | async-start | bytes 7864320 | tf_op jit(solution)/shard_map/reduce_scatter | solution.py:187
  82.3 270.6 %reduce-scatter.24.cloned.1.call-start = ((), (), s32[]{:S(2)}) async-start(), calls=%async_computation.15 | async-start | bytes 2621440 | tf_op jit(solution)/shard_map/reduce_scatter | solution.py:189
  87.2 307.7 %reduce-scatter.28.cloned.1.call-start = ((), (), s32[]{:S(2)}) async-start(), calls=%async_computation.18 | async-start | bytes 368640 | tf_op jit(solution)/shard_map/reduce_scatter | solution.py:173
  89.1 358.8 %all-reduce.7.cloned.1.call-start = ((), (), s32[]{:S(2)}) async-start(), calls=%async_computation.19 | async-start | bytes 1310720
  133.4 173.2 %copy-start.32 = (u32[32]{0:T(128)S(1)}, u32[32]{0:T(128)}, u32[]{:S(2)}) copy-start(u32[32]{0:T(128)} %constant.16) | copy-start | bytes 388
  133.4 351.9 %reduce-scatter.18.cloned.1.call-start = ((), (), s32[]{:S(2)}) async-start(), calls=%async_computation.12 | async-start | bytes 884736 | tf_op jit(solution)/shard_map/reduce_scatter | solution.py:170
  193.6 116.4 %copy-start.5 = (bf16[3,256,512]{2,1,0:T(8,128)(2,1)S(1)}, bf16[3,256,512]{2,1,0:T(8,128)(2,1)}, u32[]{:S(2)}) copy-start(bf16[3,256,512]{2,1,0:T(8,128)(2,1)} %copy-done.4) | copy-start | bytes 2359300
  193.7 333.4 %reduce-scatter.14.cloned.1.call-start = ((), (), s32[]{:S(2)}) async-start(), calls=%async_computation.10 | async-start | bytes 1769472 | tf_op jit(solution)/shard_map/reduce_scatter | solution.py:192
  306.5 356.8 %all-reduce.5.cloned.1.call-start = ((), (), s32[]{:S(2)}) async-start(), calls=%async_computation.17 | async-start | bytes 2097152 | tf_op jit(solution)/shard_map/psum | solution.py:199
  311.6 388.5 %reduce-scatter.26.cloned.1.call-start = ((), (), s32[]{:S(2)}) async-start(), calls=%async_computation.16 | async-start | bytes 589824 | tf_op jit(solution)/shard_map/reduce_scatter | solution.py:194
  311.7 8.5 %collective-permute-start.6 = (bf16[3,1,1024]{2,1,0:T(2,128)(2,1)S(1)}, bf16[3,1,1024]{2,1,0:T(2,128)(2,1)S(1)}, u32[]{:S(2)}, u32[]{:S(2)}) collective-permute-start(bf16[3,1,1024]{2,1,0:T(2,128)(2,1)S(1)} %get-tuple-element.37), channel_id=1, source_target_pairs={{1,0},{2,1},{3,2},{5,4},{6,5},{7,6},{9,8},{10,9},{11,10},{13,12},{... | collective-permute-start | bytes 18440 | tf_op jit(solution)/shard_map/ppermute | solution.py:17
  315.2 7.2 %collective-permute-start.7 = (bf16[3,1,1024]{2,1,0:T(2,128)(2,1)S(1)}, bf16[3,1,1024]{2,1,0:T(2,128)(2,1)S(1)}, u32[]{:S(2)}, u32[]{:S(2)}) collective-permute-start(bf16[3,1,1024]{2,1,0:T(2,128)(2,1)S(1)} %get-tuple-element.36), channel_id=1, source_target_pairs={{0,1},{1,2},{2,3},{4,5},{5,6},{6,7},{8,9},{9,10},{10,11},{12,13},{... | collective-permute-start | bytes 18440 | tf_op jit(solution)/shard_map/ppermute | solution.py:14
  324.8 28.1 %copy-start.28 = (f32[4,512]{1,0:T(4,128)S(1)}, f32[4,512]{1,0:T(4,128)}, u32[]{:S(2)}) copy-start(f32[4,512]{1,0:T(4,128)} %param.10) | copy-start | bytes 24580
  448.9 253.4 %copy-start.1 = (bf16[1,512,1024]{2,1,0:T(8,128)(2,1)S(1)}, bf16[1,512,1024]{2,1,0:T(8,128)(2,1)}, u32[]{:S(2)}) copy-start(bf16[1,512,1024]{2,1,0:T(8,128)(2,1)} %param.13) | copy-start | bytes 3145732
  (31 other events, 97.9 us)
Sparse Core Ops, SparseCore 0:
  47.2 30.5 reduce-scatter.21
  80.1 51.1 reduce-scatter.19
  133.6 59.9 reduce-scatter.15
  195.8 110.6 reduce-scatter.11
  308.7 44.2 reduce-scatter.23
  356.4 33.1 reduce-scatter.27
  392.7 55.2 all-reduce.6
  451.0 34.2 reduce-scatter.17
  488.6 38.3 reduce-scatter.13
  532.6 130.6 all-reduce.4
  667.0 33.0 reduce-scatter.25
where the time goes:
time: 710 us; the launch traced here: 709 us
  waiting for transfers between devices  546 us (77%)
  matrix products  53.1 us (7%)
  blocking collectives  39.9 us (6%)
  starting transfers between devices  25.3 us (4%)
  between operations  17.2 us (2%)
  local copies, waits for them, and re-layouts  15.9 us (2%)
  other arithmetic  11.9 us (2%)
    psum x1, waiting for transfers between devices, shards(): lax.psum((last_grad, end_grad, start_grad), ('dp', 'tm'))  135 us
    reduce_scatter x1, waiting for transfers between devices, shards(): lax.psum_scatter(jnp.stack(in_grads[:-1]), 'tm', scatter_dimension=3, til...  113 us
    reduce_scatter x1, waiting for transfers between devices, shards(): lax.psum_scatter(in_grads[layer_index].astype(jnp.bfloat16), 'tm', scatte...  60.1 us
    unnamed x12, waiting for transfers between devices  52.4 us
    reduce_scatter x1, waiting for transfers between devices, shards(): lax.psum_scatter(jnp.stack(cond_grads[:-1]), 'tm', scatter_dimension=2, t...  42.2 us
    reduce_scatter x1, waiting for transfers between devices, shards(): lax.psum_scatter(lower_part[0], 'dp', scatter_dimension=2, tiled=True)  40.8 us
    psum x1, blocking collectives, shards(): batch_loss = lax.psum(local_loss, ('dp', 'tm'))  39.9 us
    reduce_scatter x1, waiting for transfers between devices, shards(): lax.psum_scatter(lower_part[2], 'dp', scatter_dimension=1, tiled=True)  36.8 us
  transfers between devices with their start and end apart: 19, of which 10 were waited for; matrix products, arithmetic and copies ran while one was open for 8% of the time, Pallas kernels for 0%

commit v1 on v0

--- a/solution.py
+++ b/solution.py
@@ -1,6 +1,7 @@
 import jax
 import jax.numpy as jnp
 from jax import lax
+from jax.experimental.layout import Layout, with_layout_constraint
 from jax.sharding import PartitionSpec as P
 
 highest = lax.Precision.HIGHEST
@@ -100,7 +101,6 @@
         + 0.5 * jnp.sum(latent_rows * latent_rows)
         - jnp.sum(log_scale)
     ) * scale_inv
-    batch_loss = lax.psum(local_loss, ("dp", "tm"))
     grad_out = jnp.concatenate(
         [(latent_rows * growth * second_half - 1.0) * scale_inv, latent_rows * scale_inv], axis=-1
     ).astype(jnp.bfloat16)
@@ -113,7 +113,23 @@
     cond_grads = [None] * layers
     res_grads = [None] * (layers - 1)
     last_grad = None
-    upper_sums = None
+    clip_sums = [None] * layers
+    dp_size = lax.axis_size("dp")
+    tm_size = lax.axis_size("tm")
+
+    def by_clip_owner(grad):
+        return grad.astype(jnp.bfloat16).reshape(dp_size, -1, grad.shape[1])
+
+    def folded(grad):
+        rows, columns = grad.shape
+        halves = grad.astype(jnp.bfloat16).reshape(dp_size, 2, rows // dp_size // 2, columns)
+        return jnp.transpose(halves, (0, 2, 1, 3)).reshape(rows // 2, 2 * columns)
+
+    def unfolded(grad):
+        rows, columns = grad.shape
+        halves = grad.reshape(dp_size, rows // dp_size, 2, columns // 2)
+        return jnp.transpose(halves, (0, 2, 1, 3)).reshape(2 * rows, columns // 2)
+
     for layer_index in reversed(range(layers)):
         spread = 2**layer_index
         padded, pre_act, gated_out = stored[layer_index]
@@ -133,8 +149,7 @@
                 "cti,ctj->ij", gated_out, joined, preferred_element_type=jnp.float32
             )
         pre_back = gated_back(pre_act, act_back, channels).astype(jnp.bfloat16)
-        in_grads[layer_index] = jnp.stack(
-            [
+        in_grads[layer_index] = [
                 jnp.einsum(
                     "cti,cto->io",
                     padded[:, tap_index * spread : tap_index * spread + frames_dev],
@@ -143,7 +158,6 @@
                 )
                 for tap_index in range(taps)
             ]
-        )
         cond_grads[layer_index] = jnp.einsum(
             "ctm,cto->mo", mel_frames, pre_back, preferred_element_type=jnp.float32
         )
@@ -151,29 +165,16 @@
         state_back = state_back + dilated_back(
             grad_pad, input_weight[layer_index], spread, frames_dev
         )
+        pieces = in_grads[layer_index] + [cond_grads[layer_index]]
         if layer_index == layers - 1:
-            upper_part = (
-                lax.psum_scatter(
-                    in_grads[layer_index].astype(jnp.bfloat16),
-                    "tm",
-                    scatter_dimension=2,
-                    tiled=True,
-                ).astype(jnp.float32),
-                lax.psum_scatter(
-                    cond_grads[layer_index].astype(jnp.bfloat16),
-                    "tm",
-                    scatter_dimension=1,
-                    tiled=True,
-                ).astype(jnp.float32),
-            )
-            upper_sums = (
-                lax.psum_scatter(
-                    upper_part[0].astype(jnp.bfloat16), "dp", scatter_dimension=1, tiled=True
-                ).astype(jnp.float32),
-                lax.psum_scatter(
-                    upper_part[1].astype(jnp.bfloat16), "dp", scatter_dimension=0, tiled=True
-                ).astype(jnp.float32),
-            )
+            pieces.append(folded(last_grad))
+        else:
+            pieces.append(res_grads[layer_index])
+        packed = jnp.concatenate([by_clip_owner(piece) for piece in pieces], axis=1)
+        packed = with_layout_constraint(packed, Layout(major_to_minor=(0, 1, 2)))
+        clip_sums[layer_index] = lax.psum_scatter(
+            packed, "dp", scatter_dimension=0, tiled=True
+        )[0]
     start_grad = jnp.einsum("cth,ctk->hk", first_half, state_back, precision=highest)
     first_back = (
         jnp.einsum("ctk,hk->cth", state_back, start_weight, precision=highest)
@@ -183,20 +184,44 @@
         jnp.concatenate([first_back, latent_rows * growth * scale_inv], axis=-1), (0, 2, 1)
     )
     latent = jnp.transpose(latent_rows, (0, 2, 1))
-    lower_part = (
-        lax.psum_scatter(jnp.stack(in_grads[:-1]), "tm", scatter_dimension=3, tiled=True),
-        lax.psum_scatter(jnp.stack(cond_grads[:-1]), "tm", scatter_dimension=2, tiled=True),
-        lax.psum_scatter(jnp.stack(res_grads), "tm", scatter_dimension=2, tiled=True),
-    )
-    lower_sums = (
-        lax.psum_scatter(lower_part[0], "dp", scatter_dimension=2, tiled=True),
-        lax.psum_scatter(lower_part[1], "dp", scatter_dimension=1, tiled=True),
-        lax.psum_scatter(lower_part[2], "dp", scatter_dimension=1, tiled=True),
-    )
-    in_grad = jnp.concatenate([lower_sums[0], upper_sums[0][None]], axis=0)
-    cond_grad = jnp.concatenate([lower_sums[1], upper_sums[1][None]], axis=0)
-    res_grad = lower_sums[2]
-    last_total, end_total, start_total = lax.psum((last_grad, end_grad, start_grad), ("dp", "tm"))
+    small = jnp.concatenate(
+        [end_grad.reshape(-1), start_grad.reshape(-1), local_loss.reshape(1)]
+    )
+    small = lax.psum(lax.psum(small, "tm"), "dp")
+    end_total = small[: end_grad.size].reshape(end_grad.shape)
+    start_total = small[end_grad.size : end_grad.size + start_grad.size].reshape(start_grad.shape)
+    batch_loss = small[-1]
+    grad_rows = clip_sums[-1].shape[0] - channels // dp_size // 2
+    last_parts = lax.all_gather(clip_sums[-1][grad_rows:], "tm")
+    last_rows = jnp.sum(last_parts.astype(jnp.float32), axis=0).astype(jnp.bfloat16)
+    last_total = unfolded(lax.all_gather(last_rows, "dp", tiled=True)).astype(jnp.float32)
+    clip_sums = clip_sums[:-1] + [clip_sums[-1][:grad_rows]]
+    clip_sums, end_total, start_total, batch_loss, last_total = lax.optimization_barrier(
+        (clip_sums, end_total, start_total, batch_loss, last_total)
+    )
+    rows_all = jnp.concatenate(clip_sums, axis=0)
+    width = rows_all.shape[1] // tm_size
+    by_frame_owner = jnp.stack(
+        [rows_all[:, at * width : (at + 1) * width] for at in range(tm_size)]
+    )
+    by_frame_owner = with_layout_constraint(by_frame_owner, Layout(major_to_minor=(0, 1, 2)))
+    mine = lax.psum_scatter(by_frame_owner, "tm", scatter_dimension=0, tiled=True)[0]
+    mine = mine.astype(jnp.float32)
+    in_sums, cond_sums, res_sums, taken = [], [], [], 0
+    for layer_index in range(layers):
+        rows = taps * channels // dp_size
+        in_sums.append(mine[taken : taken + rows].reshape(taps, channels // dp_size, width))
+        taken += rows
+        rows = mel_frames.shape[2] // dp_size
+        cond_sums.append(mine[taken : taken + rows])
+        taken += rows
+        if layer_index < layers - 1:
+            rows = channels // dp_size
+            res_sums.append(mine[taken : taken + rows])
+            taken += rows
+    in_grad = jnp.stack(in_sums)
+    cond_grad = jnp.stack(cond_sums)
+    res_grad = jnp.stack(res_sums)
     return (
         latent,
         audio_grad,

time: 710 us -> 226 us (0.32)
  waiting for transfers between devices: 546 us -> 28.5 us
  blocking collectives: 39.9 us -> 67.5 us
  local copies, waits for them, and re-layouts: 15.9 us -> 31 us
    reduce_scatter x9 -> x3, waiting for transfers between devices: 356 us -> 25.4 us  [the longest x1 25.4 us: shards(): lax.psum_scatter(by_frame_owner, 'tm', scatter_dimension=0, tiled=True)[0]]
    psum x1 -> x0, waiting for transfers between devices: 135 us -> none  [shards(): lax.psum((last_grad, end_grad, start_grad), ('dp', 'tm'))]
    unnamed x12 -> x3, waiting for transfers between devices: 52.4 us -> 0.05 us
    all_gather x0 -> x2, blocking collectives: none -> 25.7 us  [the longest x1 13.9 us: shards(): last_parts = lax.all_gather(clip_sums[-1][grad_rows:], 'tm')]
    unnamed x77 -> x73, local copies, waits for them, and re-layouts: 13 us -> 15.4 us
    psum x1 -> x2, blocking collectives: 39.9 us -> 41.7 us  [shards(): small = lax.psum(lax.psum(small, 'tm'), 'dp')]
  transfers between devices with their start and end apart: 19 -> 11, of which waited for: 10 -> 2; matrix products, arithmetic and copies ran while one was open for 8% -> 21% of each run, Pallas kernels for 0% -> 0%
where the time goes in v1:
time: 226 us; the launch traced here: 225 us
  blocking collectives  67.5 us (30%)
  matrix products  48.9 us (22%)
  local copies, waits for them, and re-layouts  31 us (14%)
  waiting for transfers between devices  28.5 us (13%)
  starting transfers between devices  25.3 us (11%)
  between operations  16.4 us (7%)
  other arithmetic  7.3 us (3%)
    psum x2, blocking collectives, shards(): small = lax.psum(lax.psum(small, 'tm'), 'dp')  41.7 us
    reduce_scatter x1, waiting for transfers between devices, shards(): lax.psum_scatter(by_frame_owner, 'tm', scatter_dimension=0, tiled=True)[0]  25.4 us
    ppermute x4, starting transfers between devices, with_halo(): lax.ppermute(lax.slice_in_dim(block, block.shape[dim] - width, None, axis...  19.7 us
    unnamed x73, local copies, waits for them, and re-layouts  15.4 us
    dot_general x6, matrix products, dilated_back(): jnp.einsum('cto,io->cti', window, weight[tap_index], preferred_element_ty...  15.2 us
    all_gather x1, blocking collectives, shards(): last_parts = lax.all_gather(clip_sums[-1][grad_rows:], 'tm')  13.9 us
    dot_general x11, matrix products, project(): jnp.einsum('cti,io->cto', values, weight, preferred_element_type=jnp.floa...  11.9 us
    all_gather x1, blocking collectives, shards(): lax.all_gather(last_rows, 'dp', tiled=True)  11.8 us
  transfers between devices with their start and end apart: 11, of which 2 were waited for; matrix products, arithmetic and copies ran while one was open for 21% of the time, Pallas kernels for 0%

profile of v1, /device:TPU:0, one launch (start us, length us, event | category | flops | bytes accessed | tf_op | source)
XLA Modules:
  0.0 224.9 jit_solution(7631894428275843401)
XLA Ops:
  7.3 2.3 %fusion.105 = (bf16[3,256,512]{2,1,0:T(8,128)(2,1)S(1)}, f32[3,256,512]{2,1,0:T(8,128)S(1)}) fusion(f32[4,512]{1,0:T(4,128)} %param.10, f32[3,8,256]{2,1,0:T(8,128)} %param.8), kind=kOutput, calls=%fused_computation.180 | convolution fusion | flops 19267584 | bytes 2379776 | tf_op jit(solution)/shard_map/cth,hk->ctk/dot_general | solution.py:78
  11.0 5.9 %collective-permute-start = (bf16[3,1,512]{2,1,0:T(2,128)(2,1)S(1)}, bf16[3,1,512]{2,1,0:T(2,128)(2,1)S(1)}, u32[]{:S(2)}, u32[]{:S(2)}) collective-permute-start(bf16[3,1,512]{2,1,0:T(2,128)(2,1)S(1)} %get-tuple-element.65), channel_id=1, source_target_pairs={{0,1},{1,2},{2,3},{4,5},{5,6},{6,7},{8,9},{9,10},{10,11},{12,13},{... | collective-permute-start | bytes 9224 | tf_op jit(solution)/shard_map/ppermute | solution.py:15
  16.8 2.7 %fusion.16 = f32[3,256,1024]{2,1,0:T(8,128)S(1)} fusion(bf16[3,256,640]{2,1,0:T(8,128)(2,1)S(1)} %copy-done.25, bf16[2,640,1024]{2,1,0:T(8,128)(2,1)} %param.12), kind=kOutput, calls=%fused_computation.54 | convolution fusion | flops 1006632960 | bytes 5439488 | tf_op jit(solution)/shard_map/cti,io->cto/dot_general | solution.py:40
  27.1 3.9 %collective-permute-start.2 = (bf16[3,2,512]{2,1,0:T(2,128)(2,1)S(1)}, bf16[3,2,512]{2,1,0:T(2,128)(2,1)S(1)}, u32[]{:S(2)}, u32[]{:S(2)}) collective-permute-start(bf16[3,2,512]{2,1,0:T(2,128)(2,1)S(1)} %get-tuple-element.63), channel_id=1, source_target_pairs={{0,1},{1,2},{2,3},{4,5},{5,6},{6,7},{8,9},{9,10},{10,11},{12,13},{... | collective-permute-start | bytes 18440 | tf_op jit(solution)/shard_map/ppermute | solution.py:15
  34.5 3.0 %collective-permute-done.3 = bf16[3,2,512]{2,1,0:T(2,128)(2,1)S(1)} collective-permute-done((bf16[3,2,512]{2,1,0:T(2,128)(2,1)S(1)}, bf16[3,2,512]{2,1,0:T(2,128)(2,1)S(1)}, u32[]{:S(2)}, u32[]{:S(2)}) %collective-permute-start.3) | collective-permute-done | bytes 6176 | tf_op jit(solution)/shard_map/ppermute | solution.py:18
  43.5 2.0 bitcast_convert_fusion.3
  45.5 2.3 %bitcast_convert_fusion = bf16[1024,640]{0,1:T(8,128)(2,1)} fusion(bf16[3,256,640]{2,1,0:T(8,128)(2,1)S(1)} %copy-done.26, bf16[3,256,512]{2,1,0:T(8,128)(2,1)S(1)} %get-tuple-element.53, bf16[3,256,512]{2,1,0:T(8,128)(2,1)S(1)} %get-tuple-element.52), kind=kOutput, calls=%fused_computation.2 | convolution fusion | flops 1010434048 | bytes 3866624 | tf_op jit(solution)/shard_map/ctm,cto->mo/dot_general | solution.py:161
  49.1 2.2 reshape_reshape.3
  51.4 2.4 %bitcast_convert_fusion.4 = bf16[512,1024]{1,0:T(8,128)(2,1)S(1)} fusion(bf16[3,256,512]{2,1,0:T(8,128)(2,1)S(1)} %fusion.11, bf16[3,2,512]{2,1,0:T(2,128)(2,1)S(1)} %collective-permute-done.2, bf16[3,256,512]{2,1,0:T(8,128)(2,1)} %copy-done.15, bf16[3,256,512]{2,1,0:T(8,128)(2,1)} %copy-done.12), kind=kOutput, calls=%fused_computation.6 | convolution fusion | flops 810549248 | bytes 3414016 | tf_op jit(solution)/shard_map/cti,cto->io/dot_general | solution.py:153
  64.6 2.2 fusion.44
  66.8 5.0 %collective-permute-start.5 = (bf16[3,2,1024]{2,1,0:T(2,128)(2,1)S(1)}, bf16[3,2,1024]{2,1,0:T(2,128)(2,1)S(1)}, u32[]{:S(2)}, u32[]{:S(2)}) collective-permute-start(bf16[3,2,1024]{2,1,0:T(2,128)(2,1)S(1)} %get-tuple-element.56), channel_id=1, source_target_pairs={{0,1},{1,2},{2,3},{4,5},{5,6},{6,7},{8,9},{9,10},{10,11},{12,13},{... | collective-permute-start | bytes 36872 | tf_op jit(solution)/shard_map/ppermute | solution.py:15
  71.8 2.4 %fusion.6 = f32[3,256,512]{2,1,0:T(8,128)S(1)} fusion(bf16[3,2,1024]{2,1,0:T(2,128)(2,1)S(1)} %collective-permute-done.4, bf16[3,256,512]{2,1,0:T(8,128)(2,1)S(1)} %copy-done.17, bf16[3,256,512]{2,1,0:T(8,128)(2,1)S(1)} %copy-done.14, bf16[2,3,512,1024]{3,2,1,0:T(8,128)(2,1)} %param.11), kind=kOutput, calls=%fused_computation.24 | convolution fusion | flops 810024960 | bytes 4206592 | tf_op jit(solution)/shard_map/cto,io->cti/dot_general | solution.py:58
  74.2 3.6 %fusion.106 = (bf16[3,256,512]{2,1,0:T(8,128)(2,1)S(1)}, f32[3,256,512]{2,1,0:T(8,128)}) fusion(bf16[2,3,512,1024]{3,2,1,0:T(8,128)(2,1)} %param.11, bf16[3,2,1024]{2,1,0:T(2,128)(2,1)S(1)} %collective-permute-done.5, bf16[3,256,512]{2,1,0:T(8,128)(2,1)S(1)} %copy-done.17, bf16[3,256,512]{2,1,0:T(8,128)(2,1)S(1)} %copy-done.14, ...), kind=kOutput, calls=%fused_computation.181 | convolution fusion | flops 811204608 | bytes 8138752 | tf_op jit(solution)/shard_map/cto,io->cti/dot_general | solution.py:58
  95.9 2.5 %fusion.30 = f32[3,256,512]{2,1,0:T(8,128)S(1)} fusion(bf16[2,3,512,1024]{3,2,1,0:T(8,128)(2,1)} %param.11, bf16[3,256,512]{2,1,0:T(8,128)(2,1)} %copy-done.10, bf16[3,256,512]{2,1,0:T(8,128)(2,1)S(1)} %get-tuple-element.50), kind=kOutput, calls=%fused_computation.68 | convolution fusion | flops 808452096 | bytes 4194304 | tf_op jit(solution)/shard_map/cto,io->cti/dot_general | solution.py:58
  98.4 5.0 %collective-permute-start.7 = (bf16[3,1,1024]{2,1,0:T(2,128)(2,1)S(1)}, bf16[3,1,1024]{2,1,0:T(2,128)(2,1)S(1)}, u32[]{:S(2)}, u32[]{:S(2)}) collective-permute-start(bf16[3,1,1024]{2,1,0:T(2,128)(2,1)S(1)} %get-tuple-element.54), channel_id=1, source_target_pairs={{0,1},{1,2},{2,3},{4,5},{5,6},{6,7},{8,9},{9,10},{10,11},{12,13},{... | collective-permute-start | bytes 18440 | tf_op jit(solution)/shard_map/ppermute | solution.py:15
  103.4 2.2 fusion.2
  105.6 2.3 %add_add_fusion.2 = f32[3,256,512]{2,1,0:T(8,128)S(1)} fusion(f32[3,256,512]{2,1,0:T(8,128)S(1)} %copy-done.28, f32[3,256,512]{2,1,0:T(8,128)S(1)} %fusion.2, f32[3,256,512]{2,1,0:T(8,128)S(1)} %fusion.30, bf16[3,1,1024]{2,1,0:T(2,128)(2,1)S(1)} %collective-permute-done.7, bf16[3,256,512]{2,1,0:T(8,128)(2,1)S(1)} %copy-done.11, ...), kind=kOutput, calls=%fused_computation.44 | convolution fusion | flops 811204608 | bytes 8919040 | tf_op jit(solution)/shard_map/cto,io->cti/dot_general | solution.py:58
  108.9 18.8 %psum.14 = f32[6145]{0:T(1024)S(1)} all-reduce(f32[6145]{0:T(1024)S(1)} %pad_maximum_fusion.40), channel_id=1, replica_groups=mesh['dp'=8,'tm'=4] {'tm'}, use_global_device_ids=true, to_apply=%region_5.0 | all-reduce | flops 6145 | bytes 49160 | tf_op jit(solution)/shard_map/psum | solution.py:190
  127.7 23.0 %psum.15 = f32[6145]{0:T(1024)S(1)} all-reduce(f32[6145]{0:T(1024)S(1)} %psum.14), channel_id=1, replica_groups=mesh['dp'=8,'tm'=4] {'dp'}, use_global_device_ids=true, to_apply=%region_6.0 | all-reduce | flops 6145 | bytes 49160 | tf_op jit(solution)/shard_map/psum | solution.py:190
  152.8 13.9 %all_gather.7 = bf16[4,32,1024]{2,1,0:T(8,128)(2,1)S(1)} all-gather(bf16[1,32,1024]{2,1,0:T(8,128)(2,1)S(1)} %slice.256), channel_id=1, replica_groups=mesh['dp'=8,'tm'=4] {'tm'}, dimensions={0}, use_global_device_ids=true | all-gather | bytes 327680 | tf_op jit(solution)/shard_map/all_gather | solution.py:195
  166.8 11.8 %all_gather.8 = bf16[256,1024]{1,0:T(8,128)(2,1)S(1)} all-gather(bf16[32,1024]{1,0:T(8,128)(2,1)S(1)} %reduce_sum.42), channel_id=1, replica_groups=mesh['dp'=8,'tm'=4] {'dp'}, dimensions={0}, use_global_device_ids=true | all-gather | bytes 589824 | tf_op jit(solution)/shard_map/all_gather | solution.py:197
  178.6 1.9 reshape.111
  180.5 2.4 %copy.67 = f32[8,2,32,512]{3,2,1,0:T(8,128)} copy(f32[8,2,32,512]{3,1,2,0:T(2,128)} %bitcast.199) | data formatting | bytes 2097152 | tf_op jit(solution)/shard_map/convert_element_type | solution.py:197
  188.3 25.4 %reduce-scatter.8.cloned.1.call-done = bf16[1,608,256]{2,1,0:T(8,128)(2,1)} async-done(((bf16[4,608,256]{2,1,0:T(8,128)(2,1)}), bf16[1,608,256]{2,1,0:T(8,128)(2,1)}) %reduce-scatter.8.cloned.1.call-update) | async-done | bytes 311312 | tf_op jit(solution)/shard_map/reduce_scatter | solution.py:208
  (147 shorter events, 59.4 us)
Async XLA Ops:
  7.2 18.5 %copy-start = (bf16[1,512,1024]{2,1,0:T(8,128)(2,1)S(1)}, bf16[1,512,1024]{2,1,0:T(8,128)(2,1)}, u32[]{:S(2)}) copy-start(bf16[1,512,1024]{2,1,0:T(8,128)(2,1)} %param.13) | copy-start | bytes 3145732
  7.2 9.6 %copy-start.25 = (bf16[3,256,640]{2,1,0:T(8,128)(2,1)S(1)}, bf16[3,256,640]{2,1,0:T(8,128)(2,1)}, u32[]{:S(2)}) copy-start(bf16[3,256,640]{2,1,0:T(8,128)(2,1)} %param.9) | copy-start | bytes 2949124
  7.2 144.8 %reduce-scatter.6.cloned.1.call-start = ((), (), s32[]{:S(2)}) async-start(), calls=%async_computation.4 | async-start | bytes 5603328 | tf_op jit(solution)/shard_map/reduce_scatter | solution.py:175
  7.2 13.7 %slice-start = ((s8[6291456]{0:T(1024)(128)(4,1)}), s8[4194304]{0:T(1024)(128)(4,1)S(1)}, s32[]{:S(2)}) async-start(s8[6291456]{0:T(1024)(128)(4,1)} %bitcast.197), calls=%async_computation.6 | async-start | bytes 8388608
  9.6 13.3 %collective-permute-start.1 = (bf16[3,1,512]{2,1,0:T(2,128)(2,1)S(1)}, bf16[3,1,512]{2,1,0:T(2,128)(2,1)S(1)}, u32[]{:S(2)}, u32[]{:S(2)}) collective-permute-start(bf16[3,1,512]{2,1,0:T(2,128)(2,1)S(1)} %get-tuple-element.64), channel_id=1, source_target_pairs={{1,0},{2,1},{3,2},{5,4},{6,5},{7,6},{9,8},{10,9},{11,10},{13,12},{... | collective-permute-start | bytes 9224 | tf_op jit(solution)/shard_map/ppermute | solution.py:18
  10.9 8.6 %copy-start.24 = (bf16[2,640,1024]{2,1,0:T(8,128)(2,1)S(1)}, bf16[2,640,1024]{2,1,0:T(8,128)(2,1)}, u32[]{:S(2)}) copy-start(bf16[2,640,1024]{2,1,0:T(8,128)(2,1)} %param.12) | copy-start | bytes 7864324
  10.9 10.0 %slice-start.1 = ((s8[6291456]{0:T(1024)(128)(4,1)}), s8[2097152]{0:T(1024)(128)(4,1)S(1)}, s32[]{:S(2)}) async-start(s8[6291456]{0:T(1024)(128)(4,1)} %bitcast.197), calls=%async_computation.7 | async-start | bytes 4194304
  11.0 11.0 %collective-permute-start = (bf16[3,1,512]{2,1,0:T(2,128)(2,1)S(1)}, bf16[3,1,512]{2,1,0:T(2,128)(2,1)S(1)}, u32[]{:S(2)}, u32[]{:S(2)}) collective-permute-start(bf16[3,1,512]{2,1,0:T(2,128)(2,1)S(1)} %get-tuple-element.65), channel_id=1, source_target_pairs={{0,1},{1,2},{2,3},{4,5},{5,6},{6,7},{8,9},{9,10},{10,11},{12,13},{... | collective-permute-start | bytes 9224 | tf_op jit(solution)/shard_map/ppermute | solution.py:15
  27.1 6.4 %collective-permute-start.2 = (bf16[3,2,512]{2,1,0:T(2,128)(2,1)S(1)}, bf16[3,2,512]{2,1,0:T(2,128)(2,1)S(1)}, u32[]{:S(2)}, u32[]{:S(2)}) collective-permute-start(bf16[3,2,512]{2,1,0:T(2,128)(2,1)S(1)} %get-tuple-element.63), channel_id=1, source_target_pairs={{0,1},{1,2},{2,3},{4,5},{5,6},{6,7},{8,9},{9,10},{10,11},{12,13},{... | collective-permute-start | bytes 18440 | tf_op jit(solution)/shard_map/ppermute | solution.py:15
  32.0 5.5 %collective-permute-start.3 = (bf16[3,2,512]{2,1,0:T(2,128)(2,1)S(1)}, bf16[3,2,512]{2,1,0:T(2,128)(2,1)S(1)}, u32[]{:S(2)}, u32[]{:S(2)}) collective-permute-start(bf16[3,2,512]{2,1,0:T(2,128)(2,1)S(1)} %get-tuple-element.62), channel_id=1, source_target_pairs={{1,0},{2,1},{3,2},{5,4},{6,5},{7,6},{9,8},{10,9},{11,10},{13,12},{... | collective-permute-start | bytes 18440 | tf_op jit(solution)/shard_map/ppermute | solution.py:18
  42.9 2.6 %copy-start.12 = (bf16[3,256,512]{2,1,0:T(8,128)(2,1)}, bf16[3,256,512]{2,1,0:T(8,128)(2,1)S(1)}, u32[]{:S(2)}) copy-start(bf16[3,256,512]{2,1,0:T(8,128)(2,1)S(1)} %get-tuple-element.52) | copy-start | bytes 2359300
  42.9 2.6 %copy-start.15 = (bf16[3,256,512]{2,1,0:T(8,128)(2,1)}, bf16[3,256,512]{2,1,0:T(8,128)(2,1)S(1)}, u32[]{:S(2)}) copy-start(bf16[3,256,512]{2,1,0:T(8,128)(2,1)S(1)} %get-tuple-element.53) | copy-start | bytes 2359300
  61.3 121.7 %reduce-scatter.4.cloned.1.call-start = ((), (), s32[]{:S(2)}) async-start(), calls=%async_computation.3 | async-start | bytes 6193152 | tf_op jit(solution)/shard_map/reduce_scatter | solution.py:175
  63.3 8.5 %collective-permute-start.4 = (bf16[3,2,1024]{2,1,0:T(2,128)(2,1)S(1)}, bf16[3,2,1024]{2,1,0:T(2,128)(2,1)S(1)}, u32[]{:S(2)}, u32[]{:S(2)}) collective-permute-start(bf16[3,2,1024]{2,1,0:T(2,128)(2,1)S(1)} %get-tuple-element.57), channel_id=1, source_target_pairs={{1,0},{2,1},{3,2},{5,4},{6,5},{7,6},{9,8},{10,9},{11,10},{13,12},{... | collective-permute-start | bytes 36872 | tf_op jit(solution)/shard_map/ppermute | solution.py:18
  66.8 7.4 %collective-permute-start.5 = (bf16[3,2,1024]{2,1,0:T(2,128)(2,1)S(1)}, bf16[3,2,1024]{2,1,0:T(2,128)(2,1)S(1)}, u32[]{:S(2)}, u32[]{:S(2)}) collective-permute-start(bf16[3,2,1024]{2,1,0:T(2,128)(2,1)S(1)} %get-tuple-element.56), channel_id=1, source_target_pairs={{0,1},{1,2},{2,3},{4,5},{5,6},{6,7},{8,9},{9,10},{10,11},{12,13},{... | collective-permute-start | bytes 36872 | tf_op jit(solution)/shard_map/ppermute | solution.py:15
  74.2 3.6 %copy-start.2 = (f32[3,256,1024]{2,1,0:T(8,128)S(1)}, f32[3,256,1024]{2,1,0:T(8,128)}, u32[]{:S(2)}) copy-start(f32[3,256,1024]{2,1,0:T(8,128)} %copy-done.1) | copy-start | bytes 9437188
  74.2 3.6 %copy-start.9 = (bf16[3,256,512]{2,1,0:T(8,128)(2,1)S(1)}, bf16[3,256,512]{2,1,0:T(8,128)(2,1)}, u32[]{:S(2)}) copy-start(bf16[3,256,512]{2,1,0:T(8,128)(2,1)} %copy-done.8) | copy-start | bytes 2359300
  79.4 6.5 %copy-start.10 = (bf16[3,256,512]{2,1,0:T(8,128)(2,1)}, bf16[3,256,512]{2,1,0:T(8,128)(2,1)S(1)}, u32[]{:S(2)}) copy-start(bf16[3,256,512]{2,1,0:T(8,128)(2,1)S(1)} %get-tuple-element.51) | copy-start | bytes 2359300
  91.1 122.6 %reduce-scatter.8.cloned.1.call-start = ((), (), s32[]{:S(2)}) async-start(), calls=%async_computation.5 | async-start | bytes 1556480 | tf_op jit(solution)/shard_map/reduce_scatter | solution.py:208
  94.4 8.9 %copy-start.11 = (bf16[3,256,512]{2,1,0:T(8,128)(2,1)S(1)}, bf16[3,256,512]{2,1,0:T(8,128)(2,1)}, u32[]{:S(2)}) copy-start(bf16[3,256,512]{2,1,0:T(8,128)(2,1)} %copy-done.10) | copy-start | bytes 2359300
  94.5 8.9 %collective-permute-start.6 = (bf16[3,1,1024]{2,1,0:T(2,128)(2,1)S(1)}, bf16[3,1,1024]{2,1,0:T(2,128)(2,1)S(1)}, u32[]{:S(2)}, u32[]{:S(2)}) collective-permute-start(bf16[3,1,1024]{2,1,0:T(2,128)(2,1)S(1)} %get-tuple-element.55), channel_id=1, source_target_pairs={{1,0},{2,1},{3,2},{5,4},{6,5},{7,6},{9,8},{10,9},{11,10},{13,12},{... | collective-permute-start | bytes 18440 | tf_op jit(solution)/shard_map/ppermute | solution.py:18
  98.4 7.3 %copy-start.28 = (f32[3,256,512]{2,1,0:T(8,128)S(1)}, f32[3,256,512]{2,1,0:T(8,128)}, u32[]{:S(2)}) copy-start(f32[3,256,512]{2,1,0:T(8,128)} %get-tuple-element.78) | copy-start | bytes 4718596
  98.4 7.2 %collective-permute-start.7 = (bf16[3,1,1024]{2,1,0:T(2,128)(2,1)S(1)}, bf16[3,1,1024]{2,1,0:T(2,128)(2,1)S(1)}, u32[]{:S(2)}, u32[]{:S(2)}) collective-permute-start(bf16[3,1,1024]{2,1,0:T(2,128)(2,1)S(1)} %get-tuple-element.54), channel_id=1, source_target_pairs={{0,1},{1,2},{2,3},{4,5},{5,6},{6,7},{8,9},{9,10},{10,11},{12,13},{... | collective-permute-start | bytes 18440 | tf_op jit(solution)/shard_map/ppermute | solution.py:15
  180.5 2.5 %copy-start.18 = (bf16[1,304,1024]{2,1,0:T(8,128)(2,1)S(1)}, bf16[1,304,1024]{2,1,0:T(8,128)(2,1)}, u32[]{:S(2)}) copy-start(bf16[1,304,1024]{2,1,0:T(8,128)(2,1)} %reduce-scatter.6.cloned.1.call-done) | copy-start | bytes 1867780
  (18 other events, 26.0 us)
Sparse Core Ops, SparseCore 0:
  61.4 54.3 reduce-scatter.5
  119.3 59.8 reduce-scatter.3
  185.7 27.9 reduce-scatter.7
